TPU v7x, 32 devices: a whole 2x2x4 slice. The times are simulated.
32 devices in a mesh: rep: 2 (over y), span: 2 (over core), seq: 4 (over z), tp: 2 (over x).
Axes of the slice: x: 2, y: 2, z: 4, core: 2. Of those that a mesh axis runs over, the one named last changes fastest.
Arguments:
- queries: bfloat16 [8, 512, 24, 128], P(('rep', 'span'), 'seq', 'tp'), parts along dimension 0, may hold values from -110 to 110
- key_states: bfloat16 [8, 512, 4, 128], P(('rep', 'span'), 'seq', 'tp'), parts along dimension 0, may hold values from -11 to 11
- value_states: bfloat16 [8, 512, 4, 128], P(('rep', 'span'), 'seq', 'tp'), parts along dimension 0, may hold values from -6 to 6
- out_weight: bfloat16 [3072, 6144], P('tp', 'seq'), may hold values from -0.109375 to 0.109375
- noise_table: float32 [64, 6144], P(None, 'tp'), may hold values from 0.5 to 2
- plan: int32 [8], P('rep'), parts along dimension 0, may hold values from 0 to 63
Outputs:
- branch_out: bfloat16 [8, 512, 6144], P(('rep', 'span'), 'seq', 'tp'), parts along dimension 0
There are 2 independent parts, one for each index of `rep`. A program takes and returns all parts, laid end to end along the dimension named above; an argument that names none is the same for every part. Nothing has to cross between parts.
All inputs are finite; a program needn't handle non-finite values.
Results may differ from a plain program's by a relative error of at most 0.014.
Values may be sent and summed in bfloat16 or wider, within the bound.
A program may use at most 128 MiB of HBM per device.

v0:
```python
import jax
import jax.numpy as jnp
from jax import lax
from jax.sharding import PartitionSpec as P


def fold_block(carried, query_rows, key_rows, value_rows, factor):
    maxima, totals, weighted = carried
    scores = (
        jnp.einsum("tkgd,skd->tkgs", query_rows, key_rows, preferred_element_type=jnp.float32)
        * factor
    )
    highest = jnp.maximum(maxima, jnp.max(scores, axis=-1))
    shrink = jnp.exp(maxima - highest)
    weights = jnp.exp(scores - highest[..., None])
    totals = totals * shrink + jnp.sum(weights, axis=-1)
    weighted = weighted * shrink[..., None] + jnp.einsum(
        "tkgs,skd->tkgd",
        weights.astype(jnp.bfloat16),
        value_rows,
        preferred_element_type=jnp.float32,
    )
    return (maxima * 0.0 + highest, totals, weighted)


def per_device(queries, key_states, value_states, out_weight, noise_table, plan):
    ch_dev, tok_dev, heads_local, head_size = queries.shape
    kv_local = key_states.shape[2]
    per_kv = heads_local // kv_local
    span_count = ch_dev * lax.axis_size("span")
    first_span = lax.axis_index("span") * ch_dev
    factor = head_size ** (-0.5)
    grouped = queries.reshape(ch_dev, tok_dev, kv_local, per_kv, head_size)
    start_max = jnp.full((ch_dev, tok_dev, kv_local, per_kv), -1e30, jnp.float32)
    start_tot = jnp.zeros((ch_dev, tok_dev, kv_local, per_kv), jnp.float32)
    start_acc = jnp.zeros((ch_dev, tok_dev, kv_local, per_kv, head_size), jnp.float32)
    span_rows = (
        lax.all_gather(key_states, "seq", axis=1, tiled=True),
        lax.all_gather(value_states, "seq", axis=1, tiled=True),
    )
    key_piece = lax.all_gather(span_rows[0], "span", axis=0, tiled=True)
    value_piece = lax.all_gather(span_rows[1], "span", axis=0, tiled=True)
    new_max = []
    new_tot = []
    new_acc = []
    for q_span in range(ch_dev):
        inner_state = (start_max[q_span], start_tot[q_span], start_acc[q_span])
        for k_span in range(span_count):

            def update(inner, q_span=q_span, k_span=k_span):
                return fold_block(
                    inner, grouped[q_span], key_piece[k_span], value_piece[k_span], factor
                )

            inner_state = lax.cond(
                k_span <= first_span + q_span, update, lambda inner: inner, inner_state
            )
        new_max.append(inner_state[0])
        new_tot.append(inner_state[1])
        new_acc.append(inner_state[2])
    attn = (
        (jnp.stack(new_acc) / jnp.stack(new_tot)[..., None])
        .reshape(ch_dev, tok_dev, heads_local * head_size)
        .astype(jnp.bfloat16)
    )
    columns = jnp.einsum(
        "ctf,fo->cto",
        lax.all_gather(attn, "seq", axis=1, tiled=True),
        out_weight,
        preferred_element_type=jnp.float32,
    )
    partial_out = lax.all_to_all(
        columns.astype(jnp.bfloat16), "seq", split_axis=1, concat_axis=2, tiled=True
    ).astype(columns.dtype)
    summed = lax.psum_scatter(
        partial_out.astype(jnp.bfloat16), "tp", scatter_dimension=2, tiled=True
    ).astype(jnp.float32)
    levels = lax.dynamic_slice_in_dim(plan, first_span, ch_dev)
    picks = (levels[:, None] == jnp.arange(noise_table.shape[0], dtype=jnp.int32)[None, :]).astype(
        jnp.float32
    )
    gates = jnp.dot(picks, noise_table, precision=lax.Precision.HIGHEST)
    return (summed * gates[:, None, :]).astype(jnp.bfloat16)


def solution(mesh):
    placed = (
        P(("rep", "span"), "seq", "tp", None),
        P(("rep", "span"), "seq", "tp", None),
        P(("rep", "span"), "seq", "tp", None),
        P("tp", "seq"),
        P(None, "tp"),
        P("rep"),
    )
    return jax.shard_map(
        per_device,
        mesh=mesh,
        in_specs=placed,
        out_specs=P(("rep", "span"), "seq", "tp"),
        check_vma=False,
    )
```

profile of v0, /device:TPU:0, one launch (start us, length us, event | category | flops | bytes accessed | tf_op | source)
XLA Modules:
  0.0 320.5 jit_solution(18199733619609409647)
XLA Ops:
  6.5 1.0 copy.63
  7.5 18.0 %all_gather.15 = bf16[2,512,2,128]{3,1,2,0:T(8,128)(2,1)} all-gather(bf16[2,128,2,128]{3,1,2,0:T(8,128)(2,1)S(1)} %copy.63), channel_id=1, replica_groups=mesh['rep'=2,'span'=2,'seq'=4,'tp'=2] {'seq'}, dimensions={1}, use_global_device_ids=true | all-gather | bytes 655360 | tf_op jit(solution)/shard_map/all_gather | solution.py:38
  25.6 0.0 all-gather.6.cloned.1.call-start
  25.6 0.9 copy.64
  26.5 17.0 %all_gather.17 = bf16[2,512,2,128]{3,1,2,0:T(8,128)(2,1)} all-gather(bf16[2,128,2,128]{3,1,2,0:T(8,128)(2,1)S(1)} %copy.64), channel_id=1, replica_groups=mesh['rep'=2,'span'=2,'seq'=4,'tp'=2] {'seq'}, dimensions={1}, use_global_device_ids=true | all-gather | bytes 655360 | tf_op jit(solution)/shard_map/all_gather | solution.py:39
  43.6 0.0 all-gather.8.cloned.1.call-start
  43.7 9.6 %all-gather.6.cloned.1.call-done = bf16[4,512,2,128]{3,1,2,0:T(8,128)(2,1)} async-done(((bf16[2,512,2,128]{3,1,2,0:T(8,128)(2,1)}), bf16[4,512,2,128]{3,1,2,0:T(8,128)(2,1)}) %all-gather.6.cloned.1.call-update) | async-done | bytes 1048592 | tf_op jit(solution)/shard_map/all_gather | solution.py:42
  53.3 6.1 %conditional.12 = (f32[128,2,6]{0,2,1:T(8,128)}, f32[128,2,6]{0,2,1:T(8,128)S(1)}, f32[128,2,6,128]{3,0,2,1:T(8,128)S(1)}) conditional(s32[]{:T(128)} %convert_element_type.70, () %tuple.93, (bf16[4,512,2,128]{3,1,2,0:T(8,128)(2,1)}, bf16[2,128,2,6,128]{4,1,3,2,0:T(8,128)(2,1)}, bf16[4,512,2,128]{3,1,2,0:T(8,128)(2,1)}) %tuple.190), branch_computations={%region_16.0_spmd, %region_17.0_spmd} | conditional | flops 409147392 | bytes 11210776 | solution.py:55
  53.3 1.7 bitcast_reduce_fusion.4
  55.0 0.6 exponential_multiply_fusion.1
  55.6 1.2 fusion.85
  56.8 0.7 fusion.104
  57.5 1.9 fusion.93
  59.4 6.2 %conditional.13 = ((f32[128,2,6]{0,2,1:T(8,128)}, f32[128,2,6]{0,2,1:T(8,128)S(1)}, f32[128,2,6,128]{3,0,2,1:T(8,128)S(1)})) conditional(s32[]{:T(128)} %convert_element_type.69, (f32[128,2,6]{0,2,1:T(8,128)}, f32[128,2,6]{0,2,1:T(8,128)S(1)}, f32[128,2,6,128]{3,0,2,1:T(8,128)S(1)}) %conditional.12, (f32[128,2,6]{0,2,1:T(8,128)}, ...), branch_computations={%region_20.0_spmd, %region_21.0_spmd} | conditional | flops 409344000 | bytes 12032032 | solution.py:55
  59.4 1.7 bitcast_reduce_fusion.5
  61.1 0.7 multiply_add_fusion.5
  61.8 0.5 fusion.107
  62.3 0.7 multiply_add_fusion.4
  63.0 0.6 copy.113
  63.6 2.0 fusion.115
  65.6 6.1 %conditional.8 = (f32[128,2,6]{0,2,1:T(8,128)}, f32[128,2,6]{0,2,1:T(8,128)S(1)}, f32[128,2,6,128]{3,0,2,1:T(8,128)S(1)}) conditional(s32[]{:T(128)} %convert_element_type.66, () %tuple.87, (bf16[4,512,2,128]{3,1,2,0:T(8,128)(2,1)}, bf16[2,128,2,6,128]{4,1,3,2,0:T(8,128)(2,1)}, bf16[4,512,2,128]{3,1,2,0:T(8,128)(2,1)}) %tuple.193), branch_computations={%region_0.0_spmd, %region_1.0_spmd} | conditional | flops 409147392 | bytes 11210776 | solution.py:55
  65.6 1.7 bitcast_reduce_fusion
  67.3 0.6 exponential_multiply_fusion
  67.9 1.2 fusion.2
  69.1 0.7 fusion.21
  69.8 1.9 fusion.10
  71.8 0.2 conditional.10
  72.0 1.5 conditional.15
  72.0 0.3 copy.68
  72.2 1.2 copy.102
  73.4 1.4 conditional.11
  73.4 0.3 copy.65
  73.7 1.2 copy.100
  74.9 0.1 div.11
  75.0 1.6 copy.73
  76.6 2.9 fusion.171
  79.6 0.0 reduce-scatter.2.cloned.1.call-start
  79.6 93.0 %all-gather.8.cloned.1.call-done = bf16[2,512,1536]{2,1,0:T(8,128)(2,1)} async-done(((bf16[2,128,1536]{2,1,0:T(8,128)(2,1)}), bf16[2,512,1536]{2,1,0:T(8,128)(2,1)}) %all-gather.8.cloned.1.call-update) | async-done | bytes 3145744 | tf_op jit(solution)/shard_map/all_gather | solution.py:68
  172.6 8.1 %fusion.168 = bf16[2,512,1536]{2,1,0:T(8,128)(2,1)S(1)} fusion(bf16[2,512,1536]{2,1,0:T(8,128)(2,1)} %all-gather.8.cloned.1.call-done, bf16[1536,1536]{1,0:T(8,128)(2,1)} %param.25), kind=kOutput, calls=%fused_computation.166 | convolution fusion | flops 4833411072 | bytes 11010048 | tf_op jit(solution)/shard_map/ctf,fo->cto/dot_general | solution.py:66
  180.7 3.2 %copy.74 = bf16[2,512,1536]{2,0,1:T(2,128)(2,1)S(1)} copy(bf16[2,512,1536]{2,1,0:T(8,128)(2,1)S(1)} %fusion.168) | data formatting | bytes 6291456 | tf_op jit(solution)/shard_map/convert_element_type | solution.py:73
  183.9 73.3 %all_to_all.18 = bf16[2,512,1536]{2,0,1:T(2,128)(2,1)S(1)} all-to-all(bf16[2,512,1536]{2,0,1:T(2,128)(2,1)S(1)} %copy.74), channel_id=1, replica_groups=mesh['rep'=2,'span'=2,'seq'=4,'tp'=2] {'seq'}, dimensions={1} | all-to-all | bytes 6291456 | tf_op jit(solution)/shard_map/all_to_all | solution.py:72
  257.2 4.1 %copy.75 = bf16[2,128,4,1536]{3,2,1,0:T(4,128)(2,1)} copy(bf16[2,128,4,1536]{3,0,1,2:T(2,128)(2,1)S(1)} %bitcast.326) | data formatting | bytes 6291456 | tf_op jit(solution)/shard_map/all_to_all | solution.py:72
  261.3 6.9 %all_to_all.16 = bf16[2,128,6144]{2,1,0:T(8,128)(2,1)} reshape(bf16[2,128,4,1536]{3,2,1,0:T(4,128)(2,1)} %copy.75) | data formatting | bytes 6291456 | tf_op jit(solution)/shard_map/all_to_all | solution.py:72
  268.3 0.6 copy-done.5
  268.9 0.1 dynamic_slice.3
  269.0 0.4 fusion.172
  269.4 41.7 %reduce-scatter.2.cloned.1.call-done = bf16[2,128,3072]{2,1,0:T(8,128)(2,1)} async-done(((bf16[2,128,6144]{2,1,0:T(8,128)(2,1)}), bf16[2,128,3072]{2,1,0:T(8,128)(2,1)}) %reduce-scatter.2.cloned.1.call-update) | async-done | bytes 1572880 | tf_op jit(solution)/shard_map/reduce_scatter | solution.py:75
  311.1 2.9 multiply_convert_fusion
  (12 shorter events, 0.1 us)
Async XLA Ops:
  6.5 262.4 %copy-start = (f32[64,3072]{1,0:T(8,128)S(1)}, f32[64,3072]{1,0:T(8,128)}, u32[]{:S(2)}) copy-start(f32[64,3072]{1,0:T(8,128)} %param.26) | copy-start | bytes 2359300
  6.5 37.2 %all-gather.4.cloned.1.call-start = ((), (), s32[]{:S(2)}) async-start(), calls=%async_computation.2 | async-start | bytes 1572864 | tf_op jit(solution)/shard_map/all_gather | solution.py:41
  25.6 27.7 %all-gather.6.cloned.1.call-start = ((), (), s32[]{:S(2)}) async-start(), calls=%async_computation.3 | async-start | bytes 1572864 | tf_op jit(solution)/shard_map/all_gather | solution.py:42
  43.6 129.0 %all-gather.8.cloned.1.call-start = ((), (), s32[]{:S(2)}) async-start(), calls=%async_computation.4 | async-start | bytes 3932160 | tf_op jit(solution)/shard_map/all_gather | solution.py:68
  79.6 231.5 %reduce-scatter.2.cloned.1.call-start = ((), (), s32[]{:S(2)}) async-start(), calls=%async_computation.5 | async-start | bytes 4718592 | tf_op jit(solution)/shard_map/reduce_scatter | solution.py:75
  268.3 0.7 copy-start.5
Sparse Core Ops, SparseCore 0:
  25.7 10.8 all-gather.3
  43.7 9.5 all-gather.5
  79.7 92.8 all-gather.7
  268.4 42.6 reduce-scatter.1
where the time goes:
time: 322 us; the launch traced here: 321 us
  waiting for transfers between devices  144 us (45%)
  blocking collectives  108 us (34%)
  local copies, waits for them, and re-layouts  22.1 us (7%)
  matrix products  19.2 us (6%)
  between operations  13.2 us (4%)
  other arithmetic  12.9 us (4%)
    all_gather x1, waiting for transfers between devices, per_device(): lax.all_gather(attn, 'seq', axis=1, tiled=True)  93 us
    all_to_all x1, blocking collectives, per_device(): lax.all_to_all(columns.astype(jnp.bfloat16), 'seq', split_axis=1, concat_...  73.3 us
    reduce_scatter x1, waiting for transfers between devices, per_device(): lax.psum_scatter(partial_out.astype(jnp.bfloat16), 'tp', scatter_dimensio...  41.7 us
    all_gather x1, blocking collectives, per_device(): lax.all_gather(key_states, 'seq', axis=1, tiled=True)  18 us
    all_gather x1, blocking collectives, per_device(): lax.all_gather(value_states, 'seq', axis=1, tiled=True)  17 us
    all_to_all x2, local copies, waits for them, and re-layouts, per_device(): lax.all_to_all(columns.astype(jnp.bfloat16), 'seq', split_axis=1, concat_...  11 us
    all_gather x1, waiting for transfers between devices, per_device(): value_piece = lax.all_gather(span_rows[1], 'span', axis=0, tiled=True)  9.6 us
    dot_general x1, matrix products, per_device(): jnp.einsum('ctf,fo->cto', lax.all_gather(attn, 'seq', axis=1, tiled=True)...  8.06 us
  transfers between devices with their start and end apart: 4, of which 3 were waited for; matrix products, arithmetic and copies ran while one was open for 0% of the time, Pallas kernels for 0%

commit v1 on v0

--- a/solution.py
+++ b/solution.py
@@ -65,7 +65,9 @@
     )
     columns = jnp.einsum(
         "ctf,fo->cto",
-        lax.all_gather(attn, "seq", axis=1, tiled=True),
+        jnp.concatenate(
+            lax.all_to_all(jnp.stack([attn] * lax.axis_size("seq")), "seq", 0, 0), axis=1
+        ),
         out_weight,
         preferred_element_type=jnp.float32,
     )

time: 322 us -> 291 us (0.904)
  waiting for transfers between devices: 144 us -> 54 us
  blocking collectives: 108 us -> 174 us
    all_gather x1 -> x0, waiting for transfers between devices: 93 us -> none  [per_device(): lax.all_gather(attn, 'seq', axis=1, tiled=True)]
    all_to_all x0 -> x1, blocking collectives: none -> 67.5 us  [per_device(): lax.all_to_all(jnp.stack([attn] * lax.axis_size('seq')), 'seq', 0, 0)]
  transfers between devices with their start and end apart: 4 -> 3, of which waited for: 3 -> 2; matrix products, arithmetic and copies ran while one was open for 0% -> 0% of each run, Pallas kernels for 0% -> 0%
where the time goes in v1:
time: 291 us; the launch traced here: 290 us
  blocking collectives  174 us (60%)
  waiting for transfers between devices  54 us (19%)
  local copies, waits for them, and re-layouts  20.6 us (7%)
  matrix products  16.4 us (6%)
  between operations  13.2 us (5%)
  other arithmetic  11.4 us (4%)
    all_to_all x1, blocking collectives, per_device(): lax.all_to_all(columns.astype(jnp.bfloat16), 'seq', split_axis=1, concat_...  71.2 us
    all_to_all x1, blocking collectives, per_device(): lax.all_to_all(jnp.stack([attn] * lax.axis_size('seq')), 'seq', 0, 0)  67.5 us
    reduce_scatter x1, waiting for transfers between devices, per_device(): lax.psum_scatter(partial_out.astype(jnp.bfloat16), 'tp', scatter_dimensio...  44.4 us
    all_gather x1, blocking collectives, per_device(): lax.all_gather(key_states, 'seq', axis=1, tiled=True)  18 us
    all_gather x1, blocking collectives, per_device(): lax.all_gather(value_states, 'seq', axis=1, tiled=True)  17 us
    all_to_all x2, local copies, waits for them, and re-layouts, per_device(): lax.all_to_all(columns.astype(jnp.bfloat16), 'seq', split_axis=1, concat_...  11 us
    all_gather x1, waiting for transfers between devices, per_device(): value_piece = lax.all_gather(span_rows[1], 'span', axis=0, tiled=True)  9.6 us
  transfers between devices with their start and end apart: 3, of which 2 were waited for; matrix products, arithmetic and copies ran while one was open for 0% of the time, Pallas kernels for 0%

profile of v1, /device:TPU:0, one launch (start us, length us, event | category | flops | bytes accessed | tf_op | source)
XLA Modules:
  0.0 289.6 jit_solution(5124503000283532018)
XLA Ops:
  6.5 1.0 copy.37
  7.5 18.0 %all_gather.12 = bf16[2,512,2,128]{3,1,2,0:T(8,128)(2,1)} all-gather(bf16[2,128,2,128]{3,1,2,0:T(8,128)(2,1)S(1)} %copy.37), channel_id=1, replica_groups=mesh['rep'=2,'span'=2,'seq'=4,'tp'=2] {'seq'}, dimensions={1}, use_global_device_ids=true | all-gather | bytes 655360 | tf_op jit(solution)/shard_map/all_gather | solution.py:38
  25.5 0.0 all-gather.3.cloned.1.call-update
  25.6 0.0 all-gather.5.cloned.1.call-start
  25.6 0.9 copy.38
  26.5 17.0 %all_gather.14 = bf16[2,512,2,128]{3,1,2,0:T(8,128)(2,1)} all-gather(bf16[2,128,2,128]{3,1,2,0:T(8,128)(2,1)S(1)} %copy.38), channel_id=1, replica_groups=mesh['rep'=2,'span'=2,'seq'=4,'tp'=2] {'seq'}, dimensions={1}, use_global_device_ids=true | all-gather | bytes 655360 | tf_op jit(solution)/shard_map/all_gather | solution.py:39
  43.6 0.0 all-gather.5.cloned.1.call-update
  43.6 0.0 reduce-scatter.2.cloned.1.call-start
  43.7 0.0 all-gather.3.cloned.1.call-done
  43.7 9.6 %all-gather.5.cloned.1.call-done = bf16[4,512,2,128]{3,1,2,0:T(8,128)(2,1)} async-done(((bf16[2,512,2,128]{3,1,2,0:T(8,128)(2,1)}), bf16[4,512,2,128]{3,1,2,0:T(8,128)(2,1)}) %all-gather.5.cloned.1.call-update) | async-done | bytes 1048592 | tf_op jit(solution)/shard_map/all_gather | solution.py:42
  53.3 6.1 %conditional.8 = (f32[128,2,6]{0,2,1:T(8,128)}, f32[128,2,6]{0,2,1:T(8,128)S(1)}, f32[128,2,6,128]{3,0,2,1:T(8,128)S(1)}) conditional(s32[]{:T(128)} %convert_element_type.68, () %tuple.87, (bf16[4,512,2,128]{3,1,2,0:T(8,128)(2,1)}, bf16[2,128,2,6,128]{4,1,3,2,0:T(8,128)(2,1)}, bf16[4,512,2,128]{3,1,2,0:T(8,128)(2,1)}) %tuple.174), branch_computations={%region_0.0_spmd, %region_1.0_spmd} | conditional | flops 409147392 | bytes 11210776 | solution.py:55
  53.3 1.7 bitcast_reduce_fusion
  55.0 0.6 exponential_multiply_fusion
  55.6 1.2 fusion.2
  56.8 0.7 fusion.21
  57.5 1.9 fusion.10
  59.4 6.1 %conditional.12 = (f32[128,2,6]{0,2,1:T(8,128)}, f32[128,2,6]{0,2,1:T(8,128)S(1)}, f32[128,2,6,128]{3,0,2,1:T(8,128)S(1)}) conditional(s32[]{:T(128)} %convert_element_type.72, () %tuple.93, (bf16[4,512,2,128]{3,1,2,0:T(8,128)(2,1)}, bf16[2,128,2,6,128]{4,1,3,2,0:T(8,128)(2,1)}, bf16[4,512,2,128]{3,1,2,0:T(8,128)(2,1)}) %tuple.177), branch_computations={%region_16.0_spmd, %region_17.0_spmd} | conditional | flops 409147392 | bytes 11210776 | solution.py:55
  59.4 1.7 bitcast_reduce_fusion.4
  61.1 0.6 exponential_multiply_fusion.1
  61.7 1.2 fusion.85
  62.9 0.7 fusion.104
  63.6 1.9 fusion.93
  65.5 6.2 %conditional.13 = ((f32[128,2,6]{0,2,1:T(8,128)}, f32[128,2,6]{0,2,1:T(8,128)S(1)}, f32[128,2,6,128]{3,0,2,1:T(8,128)S(1)})) conditional(s32[]{:T(128)} %convert_element_type.71, (f32[128,2,6]{0,2,1:T(8,128)}, f32[128,2,6]{0,2,1:T(8,128)S(1)}, f32[128,2,6,128]{3,0,2,1:T(8,128)S(1)}) %conditional.12, (f32[128,2,6]{0,2,1:T(8,128)}, ...), branch_computations={%region_20.0_spmd, %region_21.0_spmd} | conditional | flops 409344000 | bytes 12032032 | solution.py:55
  65.5 1.7 bitcast_reduce_fusion.5
  67.2 0.7 multiply_add_fusion.5
  67.9 0.5 fusion.107
  68.4 0.7 multiply_add_fusion.4
  69.1 2.0 fusion.115
  71.2 0.6 copy.82
  71.8 1.2 conditional.11
  71.8 1.2 copy.39
  72.9 1.2 conditional.15
  72.9 1.2 copy.42
  74.1 1.5 fusion.171
  75.6 0.3 copy.45
  75.9 0.3 stack.43
  76.2 67.5 %all_to_all.23 = bf16[4,2,128,1536]{3,2,1,0:T(8,128)(2,1)S(1)} all-to-all(bf16[4,2,128,1536]{3,2,1,0:T(8,128)(2,1)S(1)} %stack.43), channel_id=1, replica_groups=mesh['rep'=2,'span'=2,'seq'=4,'tp'=2] {'seq'}, dimensions={0} | all-to-all | bytes 6291456 | tf_op jit(solution)/shard_map/all_to_all | solution.py:69
  143.7 0.2 copy.46
  144.0 5.3 %fusion.168 = bf16[2,512,1536]{2,1,0:T(8,128)(2,1)S(1)} fusion(bf16[2,512,1536]{2,1,0:T(8,128)(2,1)S(1)} %bitcast.331, bf16[1536,1536]{1,0:T(8,128)(2,1)S(1)} %bitcast.335), kind=kOutput, calls=%fused_computation.166 | convolution fusion | flops 4833411072 | bytes 11010048 | tf_op jit(solution)/shard_map/ctf,fo->cto/dot_general | solution.py:66
  149.2 3.2 %copy.47 = bf16[2,512,1536]{2,0,1:T(2,128)(2,1)S(1)} copy(bf16[2,512,1536]{2,1,0:T(8,128)(2,1)S(1)} %fusion.168) | data formatting | bytes 6291456 | tf_op jit(solution)/shard_map/convert_element_type | solution.py:75
  152.5 71.2 %all_to_all.24 = bf16[2,512,1536]{2,0,1:T(2,128)(2,1)S(1)} all-to-all(bf16[2,512,1536]{2,0,1:T(2,128)(2,1)S(1)} %copy.47), channel_id=1, replica_groups=mesh['rep'=2,'span'=2,'seq'=4,'tp'=2] {'seq'}, dimensions={1} | all-to-all | bytes 6291456 | tf_op jit(solution)/shard_map/all_to_all | solution.py:74
  223.7 4.1 %copy.48 = bf16[2,128,4,1536]{3,2,1,0:T(4,128)(2,1)} copy(bf16[2,128,4,1536]{3,0,1,2:T(2,128)(2,1)S(1)} %bitcast.330) | data formatting | bytes 6291456 | tf_op jit(solution)/shard_map/all_to_all | solution.py:74
  227.8 6.9 %all_to_all.20 = bf16[2,128,6144]{2,1,0:T(8,128)(2,1)} reshape(bf16[2,128,4,1536]{3,2,1,0:T(4,128)(2,1)} %copy.48) | data formatting | bytes 6291456 | tf_op jit(solution)/shard_map/all_to_all | solution.py:74
  234.8 0.6 copy-done.5
  235.4 0.1 dynamic_slice.3
  235.5 0.4 fusion.172
  235.8 44.4 %reduce-scatter.2.cloned.1.call-done = bf16[2,128,3072]{2,1,0:T(8,128)(2,1)} async-done(((bf16[2,128,6144]{2,1,0:T(8,128)(2,1)}), bf16[2,128,3072]{2,1,0:T(8,128)(2,1)}) %reduce-scatter.2.cloned.1.call-update) | async-done | bytes 1572880 | tf_op jit(solution)/shard_map/reduce_scatter | solution.py:77
  280.2 2.9 %multiply_convert_fusion = bf16[2,128,3072]{2,1,0:T(8,128)(2,1)} fusion(bf16[2,128,3072]{2,1,0:T(8,128)(2,1)} %reduce-scatter.2.cloned.1.call-done, f32[2,3072]{1,0:T(2,128)S(1)} %fusion.172), kind=kLoop, calls=%fused_computation.167 | loop fusion | flops 2359296 | bytes 3170304 | tf_op jit(solution)/shard_map/convert_element_type | solution.py:85
  (14 shorter events, 0.1 us)
Async XLA Ops:
  6.5 228.9 %copy-start = (f32[64,3072]{1,0:T(8,128)S(1)}, f32[64,3072]{1,0:T(8,128)}, u32[]{:S(2)}) copy-start(f32[64,3072]{1,0:T(8,128)} %param.26) | copy-start | bytes 2359300
  6.5 37.2 %all-gather.3.cloned.1.call-start = ((), (), s32[]{:S(2)}) async-start(), calls=%async_computation.3 | async-start | bytes 1572864 | tf_op jit(solution)/shard_map/all_gather | solution.py:41
  25.6 27.7 %all-gather.5.cloned.1.call-start = ((), (), s32[]{:S(2)}) async-start(), calls=%async_computation.4 | async-start | bytes 1572864 | tf_op jit(solution)/shard_map/all_gather | solution.py:42
  43.6 236.6 %reduce-scatter.2.cloned.1.call-start = ((), (), s32[]{:S(2)}) async-start(), calls=%async_computation.5 | async-start | bytes 4718592 | tf_op jit(solution)/shard_map/reduce_scatter | solution.py:77
  75.9 68.0 %slice-start = ((s8[4718592]{0:T(1024)(128)(4,1)}), s8[4194304]{0:T(1024)(128)(4,1)S(1)}, s32[]{:S(2)}) async-start(s8[4718592]{0:T(1024)(128)(4,1)} %bitcast.334), calls=%async_computation.6 | async-start | bytes 8388608
  76.2 67.8 %slice-start.1 = ((s8[4718592]{0:T(1024)(128)(4,1)}), s8[524288]{0:T(1024)(128)(4,1)S(1)}, s32[]{:S(2)}) async-start(s8[4718592]{0:T(1024)(128)(4,1)} %bitcast.334), calls=%async_computation.7 | async-start | bytes 1048576
  234.7 0.7 copy-start.5
Sparse Core Ops, SparseCore 0:
  25.7 10.8 all-gather.2
  43.7 9.5 all-gather.4
  234.9 45.2 reduce-scatter.1
